TPU v7x, 256 devices: a whole 4x4x8 slice. The times are simulated.
256 devices in a mesh: dp: 8 (over z_lo, core), vocab: 32 (over z_hi, x, y).
Axes of the slice: x: 4, y: 4, z: 8 (z_hi: 2, z_lo: 4; z = z_hi * 4 + z_lo), core: 2. Of those that a mesh axis runs over, the one named last changes fastest.
Arguments:
- policy_hidden: bfloat16 [1024, 4096], P('dp'), may hold values from -84 to 84
- policy_weight: bfloat16 [4096, 65536], P('dp', 'vocab'), may hold values from -0.09375 to 0.09375
- reference_hidden: bfloat16 [1024, 4096], P(('dp', 'vocab')), may hold values from -84 to 84
- reference_weight: bfloat16 [4096, 65536], P(None, ('dp', 'vocab')), may hold values from -0.09375 to 0.09375
- targets: int32 [1024], replicated, may hold values from 0 to 65535
- response_mask: int32 [1024], replicated, may hold values 0 or 1
- pair_index: int32 [32], replicated, may hold values from 0 to 31, each once
Outputs:
- hidden_grad: bfloat16 [1024, 4096], P('vocab', 'dp')
- weight_grad: bfloat16 [4096, 65536], P('dp', 'vocab')
- total_loss: float32 [], replicated
Inputs may be any that keep to these rules, and one draw needn't show every extreme that they name: `pair_index`: each number of 0 to 31 once; entries 2p and 2p + 1 are the chosen and the rejected sequence of pair p.
All inputs are finite; a program needn't handle non-finite values.
Results may differ from a plain program's by a relative error of at most 0.005.
The roundings to bfloat16 on the way count: a program that leaves them out, or rounds other values in their place, can miss the bound.
Values may be sent and summed in bfloat16 or wider, within the bound.
A program may use at most 128 MiB of HBM per device.

v0:
```python
import jax
import jax.numpy as jnp
from jax import lax
from jax.sharding import Mesh
from jax.sharding import PartitionSpec as P

SEQ_LEN = 32
DP = ("dp_0", "dp_1")
VOCAB = ("vocab_0", "vocab_1", "vocab_2")
DP_VOCAB = ("dp_0", "dp_1", "vocab_0", "vocab_1", "vocab_2")
beta = 0.1
loss_scale = 4096.0


def all_in_one(value, axis):
    leaves = jax.tree.leaves(value)
    order = sorted(range(len(leaves)), key=lambda k: -leaves[k].size)
    width = (1, *leaves[order[0]].shape)[-1]
    lines = [
        jnp.pad(leaves[k].reshape(-1), (0, -leaves[k].size % width)).reshape(-1, width)
        for k in order
    ]
    both, at, found = (lax.all_gather(jnp.concatenate(lines), axis), 0, {})
    for k, line in zip(order, lines):
        slab = both[:, at : at + len(line)].reshape(len(both), -1)
        found[k] = slab[:, : leaves[k].size].reshape(-1, *leaves[k].shape)
        at += len(line)
    numbers = iter(range(len(leaves)))
    return jax.tree.map(lambda _: found[next(numbers)], value)


def merged_by_axis(value, axes, combine):
    for axis in axes:
        pieces = all_in_one(value, axis)
        value = jax.tree.map(lambda part: part[0], pieces)
        for k in range(1, lax.axis_size(axis)):
            value = combine(value, jax.tree.map(lambda part: part[k], pieces))
    return value


def in_blocks(value, dim, peers):
    shape = value.shape
    tiles = value.reshape(*shape[:dim], peers, shape[dim] // peers, *shape[dim + 1 :])
    return jnp.moveaxis(tiles, dim, 0)


def sum_at_owner(value, axis, dim):
    peers = lax.axis_size(axis)
    tiles = lax.all_to_all(in_blocks(value, dim, peers), axis, 0, 0, tiled=True)
    return jnp.sum(tiles, axis=0)


def pair_terms(log_ratio, pair_index):
    chosen = pair_index[0::2]
    rejected = pair_index[1::2]
    margin = beta * (log_ratio[chosen] - log_ratio[rejected])
    pair_count = chosen.shape[0]
    total_loss = jnp.sum(jax.nn.softplus(-margin)) / pair_count
    weight = -beta * loss_scale * jax.nn.sigmoid(-margin) / pair_count
    numbers = jnp.arange(log_ratio.shape[0], dtype=jnp.int32)[:, None]
    factor = jnp.sum(
        jnp.where(numbers == chosen[None, :], weight[None, :], 0.0)
        - jnp.where(numbers == rejected[None, :], weight[None, :], 0.0),
        axis=1,
    )
    return (total_loss, factor)


def local_pick(logits, targets, offset, axis):
    column_ids = lax.broadcasted_iota(jnp.int32, logits.shape, axis)
    shifted = targets - offset
    wanted = shifted[:, None] if axis == 1 else shifted[None, :]
    return jnp.sum(jnp.where(column_ids == wanted, logits, 0.0), axis=axis)


def merge_pair(earlier, later):
    largest = jnp.maximum(earlier[0], later[0])
    exp_total = earlier[1] * jnp.exp(earlier[0] - largest) + later[1] * jnp.exp(later[0] - largest)
    return (largest, exp_total, earlier[2] + later[2])


def merge_heads(earlier, later):
    return merge_pair(earlier[0:3], later[0:3]) + merge_pair(earlier[3:6], later[3:6])


def local(
    policy_hidden,
    policy_weight,
    reference_hidden,
    reference_weight,
    targets,
    response_mask,
    pair_index,
):
    data_index = lax.axis_index(DP)
    vocab_index = lax.axis_index(VOCAB)
    vocab_devices = lax.axis_size(VOCAB)
    data_devices = lax.axis_size(DP)
    policy_width = policy_weight.shape[1]
    reference_width = reference_weight.shape[1]
    active = response_mask.astype(jnp.float32)
    columns = lax.all_to_all(policy_hidden, DP, split_axis=1, concat_axis=0, tiled=True)
    reference_logits = jnp.dot(
        lax.all_gather(reference_hidden, DP_VOCAB, axis=0, tiled=True),
        reference_weight,
        preferred_element_type=jnp.float32,
    )
    reference_offset = (data_index * vocab_devices + vocab_index) * reference_width
    reference_top = jnp.max(reference_logits, axis=1)
    reference_pick = local_pick(reference_logits, targets, reference_offset, 1)
    slice_width = policy_width // data_devices
    weight_block = policy_weight
    policy_logits = lax.psum_scatter(
        lax.dot_general(
            weight_block, columns, (((0,), (1,)), ((), ())), preferred_element_type=jnp.float32
        ),
        DP,
        scatter_dimension=0,
        tiled=True,
    )
    policy_offset = vocab_index * policy_width + data_index * slice_width
    policy_top = jnp.max(policy_logits, axis=0)
    policy_pick = local_pick(policy_logits, targets, policy_offset, 0)
    local_stats = (
        policy_top,
        jnp.sum(jnp.exp(policy_logits - policy_top[None, :]), axis=0),
        policy_pick,
        reference_top,
        jnp.sum(jnp.exp(reference_logits - reference_top[:, None]), axis=1),
        reference_pick,
    )
    merged = merged_by_axis(local_stats, DP_VOCAB, merge_heads)
    policy_total = merged[0] + jnp.log(merged[1])
    reference_logp = merged[5] - merged[3] - jnp.log(merged[4])
    log_ratio = jnp.sum(
        (active * (merged[2] - policy_total - reference_logp)).reshape(-1, SEQ_LEN), axis=1
    )
    total_loss, factor = pair_terms(log_ratio, pair_index)
    token_scale = active * jnp.repeat(factor, SEQ_LEN)
    row_ids = lax.broadcasted_iota(jnp.int32, policy_logits.shape, 0)
    onehot = (row_ids == (targets - policy_offset)[None, :]).astype(jnp.float32)
    logit_grad = (
        token_scale[None, :] * (onehot - jnp.exp(policy_logits - policy_total[None, :]))
    ).astype(jnp.bfloat16)
    segment = lax.all_gather(logit_grad, DP, axis=0, tiled=True)
    weight_block = policy_weight
    column_grad = lax.dot_general(
        columns, segment, (((0,), (1,)), ((), ())), preferred_element_type=jnp.float32
    )
    hidden_part = lax.dot_general(
        segment, weight_block, (((0,), (1,)), ((), ())), preferred_element_type=jnp.float32
    )
    weight_grad, hidden_part = (column_grad, hidden_part)
    hidden_grad = sum_at_owner(hidden_part, VOCAB, 0)
    return (hidden_grad.astype(jnp.bfloat16), weight_grad.astype(jnp.bfloat16), total_loss)


def solution(mesh):
    torus = Mesh(
        mesh.devices.reshape(4, 2, 2, 4, 4), ("dp_0", "dp_1", "vocab_0", "vocab_1", "vocab_2")
    )
    in_specs = (P(DP, None), P(DP, VOCAB), P(DP_VOCAB, None), P(None, DP_VOCAB), P(), P(), P())
    out_specs = (P(VOCAB, DP), P(DP, VOCAB), P())
    return jax.shard_map(local, mesh=torus, in_specs=in_specs, out_specs=out_specs, check_vma=False)
```

profile of v0, /device:TPU:38, one launch (start us, length us, event | category | flops | bytes accessed | tf_op | source)
XLA Modules:
  0.0 990.6 jit_solution(14023371967877538093)
XLA Ops:
  8.0 0.0 all-gather.16.cloned.1.call-start
  8.1 0.7 all-gather.16.cloned.1.call-update
  8.7 0.0 reduce-scatter.2.cloned.1.call-start
  8.8 2.3 copy.18
  11.1 30.3 %all_to_all.24 = bf16[128,8,512]{0,2,1:T(8,128)(2,1)S(1)} all-to-all(bf16[128,8,512]{0,2,1:T(8,128)(2,1)} %bitcast.453), channel_id=1, replica_groups=mesh['dp_0'=4,'dp_1'=2,'vocab_0'=2,'vocab_1'=4,'vocab_2'=4] {'dp_0','dp_1'}, dimensions={1} | all-to-all | bytes 2097152 | tf_op jit(solution)/shard_map/all_to_all | solution.py:102
  41.3 1.3 copy.19
  42.6 6.8 fusion.94
  49.5 0.0 reduce-scatter.2.cloned.1.call-update
  49.5 0.0 all-gather.14.cloned.1.call-start
  49.6 0.6 copy-done.5
  50.1 0.1 slice.613
  50.2 0.1 slice.516
  50.4 675.5 %all-gather.16.cloned.1.call-done = bf16[256,4,4096]{2,1,0:T(4,128)(2,1)} async-done(((bf16[1,4,4096]{2,1,0:T(4,128)(2,1)}), bf16[256,4,4096]{2,1,0:T(4,128)(2,1)}) %all-gather.16.cloned.1.call-update) | async-done | bytes 8388624 | tf_op jit(solution)/shard_map/all_gather | solution.py:104
  725.9 12.5 %reshape.1600 = bf16[1024,4096]{1,0:T(8,128)(2,1)} reshape(bf16[256,4,4096]{2,1,0:T(4,128)(2,1)} %all-gather.16.cloned.1.call-done) | data formatting | bytes 16777216
  738.4 6.4 fusion.93
  744.8 0.3 select_reduce_fusion
  745.1 0.0 reduce-scatter.2.cloned.1.call-done
  745.1 1.3 reduce_max.18
  746.4 1.6 select_reduce_fusion.1
  748.0 0.1 concatenate.15
  748.1 59.3 %all-gather.6 = f32[4,6,1024]{2,1,0:T(8,128)S(1)} all-gather(f32[1,6,1024]{2,1,0:T(8,128)S(1)} %bitcast.457), channel_id=2, replica_groups=mesh['dp_0'=4,'dp_1'=2,'vocab_0'=2,'vocab_1'=4,'vocab_2'=4] {'dp_0'}, dimensions={0}, use_global_device_ids=true | all-gather | bytes 122880 | tf_op jit(solution)/shard_map/all_gather | solution.py:23
  807.4 0.1 fusion.39
  807.5 0.1 concatenate.16
  807.6 1.9 all-gather.7
  809.5 0.1 concatenate.17
  809.5 8.5 all-gather.8
  818.1 0.1 concatenate.18
  818.1 21.7 %all-gather.9 = f32[4,6,1024]{2,1,0:T(8,128)S(1)} all-gather(f32[1,6,1024]{2,1,0:T(8,128)S(1)} %bitcast.460), channel_id=5, replica_groups=mesh['dp_0'=4,'dp_1'=2,'vocab_0'=2,'vocab_1'=4,'vocab_2'=4] {'vocab_1'}, dimensions={0}, use_global_device_ids=true | all-gather | bytes 122880 | tf_op jit(solution)/shard_map/all_gather | solution.py:23
  839.9 0.1 fusion.3
  840.0 0.1 concatenate.19
  840.0 12.1 %all-gather.10 = f32[4,6,1024]{2,1,0:T(8,128)S(1)} all-gather(f32[1,6,1024]{2,1,0:T(8,128)S(1)} %bitcast.461), channel_id=6, replica_groups=mesh['dp_0'=4,'dp_1'=2,'vocab_0'=2,'vocab_1'=4,'vocab_2'=4] {'vocab_2'}, dimensions={0}, use_global_device_ids=true | all-gather | bytes 122880 | tf_op jit(solution)/shard_map/all_gather | solution.py:23
  852.1 0.1 fusion.92
  852.2 0.1 reshape.1573
  852.3 0.1 reduce_sum.76
  852.4 0.7 gather_fusion.1
  853.1 0.7 gather_fusion
  853.8 0.6 fusion.83
  854.4 0.1 subtract_reduce_fusion
  854.5 0.1 broadcast_in_dim.51
  854.6 0.1 reshape.1574
  854.6 1.1 multiply_convert_fusion
  855.7 50.3 %all-gather.14.cloned.1.call-done = bf16[2048,1024]{1,0:T(8,128)(2,1)} async-done(((bf16[256,1024]{1,0:T(8,128)(2,1)}), bf16[2048,1024]{1,0:T(8,128)(2,1)}) %all-gather.14.cloned.1.call-update) | async-done | bytes 4194320 | tf_op jit(solution)/shard_map/all_gather | solution.py:145
  906.1 5.9 fusion.95
  912.0 13.1 %all-to-all-start.1 = ((f32[32,32,512]{2,1,0:T(8,128)}), f32[32,32,512]{2,1,0:T(8,128)}, u32[]{:S(2)}, u32[]{:S(2)}) async-start(f32[32,32,512]{2,1,0:T(8,128)} %bitcast.454), calls=%async_computation.2 | async-start | bytes 4194304 | tf_op jit(solution)/shard_map/all_to_all | solution.py:49
  925.8 5.9 fusion
  931.7 3.9 copy.20
  935.6 44.1 %all-to-all-done.1 = f32[32,32,512]{2,1,0:T(8,128)} async-done(((f32[32,32,512]{2,1,0:T(8,128)}), f32[32,32,512]{2,1,0:T(8,128)}, u32[]{:S(2)}, u32[]{:S(2)}) %all-to-all-start.1) | async-done | bytes 2097184 | tf_op jit(solution)/shard_map/all_to_all | solution.py:49
  979.7 2.4 reduce_sum.78
  (26 shorter events, 0.3 us)
Async XLA Ops:
  8.0 34.6 %copy-start = (bf16[512,2048]{1,0:T(8,128)(2,1)S(1)}, bf16[512,2048]{1,0:T(8,128)(2,1)}, u32[]{:S(2)}) copy-start(bf16[512,2048]{1,0:T(8,128)(2,1)} %param.8) | copy-start | bytes 6291460
  8.0 717.9 %all-gather.16.cloned.1.call-start = ((), (), s32[]{:S(2)}) async-start(), calls=%async_computation.5 | async-start | bytes 8421376 | tf_op jit(solution)/shard_map/all_gather | solution.py:104
  8.7 736.4 %reduce-scatter.2.cloned.1.call-start = ((), (), s32[]{:S(2)}) async-start(), calls=%async_computation.3 | async-start | bytes 9437184 | tf_op jit(solution)/shard_map/reduce_scatter | solution.py:113
  49.5 0.7 copy-start.5
  49.5 0.9 copy-start.4
  49.5 856.6 %all-gather.14.cloned.1.call-start = ((), (), s32[]{:S(2)}) async-start(), calls=%async_computation.4 | async-start | bytes 4718592 | tf_op jit(solution)/shard_map/all_gather | solution.py:145
  745.1 107.1 %copy-start.3 = (s32[1024]{0:T(1024)S(1)}, s32[1024]{0:T(1024)}, u32[]{:S(2)}) copy-start(s32[1024]{0:T(1024)} %param.12) | copy-start | bytes 12292
  746.4 108.2 %copy-start.1 = (f32[256,1024]{1,0:T(8,128)S(1)}, f32[256,1024]{1,0:T(8,128)}, u32[]{:S(2)}) copy-start(f32[256,1024]{1,0:T(8,128)} %reduce-scatter.2.cloned.1.call-done) | copy-start | bytes 3145732
  912.0 13.8 %copy-start.2 = (bf16[8,128,512]{2,1,0:T(8,128)(2,1)S(1)}, bf16[8,128,512]{2,1,0:T(8,128)(2,1)}, u32[]{:S(2)}) copy-start(bf16[8,128,512]{2,1,0:T(8,128)(2,1)} %copy.19) | copy-start | bytes 3145732
  912.0 67.7 %all-to-all-start.1 = ((f32[32,32,512]{2,1,0:T(8,128)}), f32[32,32,512]{2,1,0:T(8,128)}, u32[]{:S(2)}, u32[]{:S(2)}) async-start(f32[32,32,512]{2,1,0:T(8,128)} %bitcast.454), calls=%async_computation.2 | async-start | bytes 4194304 | tf_op jit(solution)/shard_map/all_to_all | solution.py:49
Sparse Core Ops, SparseCore 0:
  10.7 715.1 all-gather.15
Sparse Core Ops, SparseCore 1:
  49.6 93.9 reduce-scatter.1
  855.8 50.2 all-gather.13
where the time goes:
time: 991 us
  waiting for transfers between devices  771 us (78%)
  blocking collectives  134 us (14%)
  matrix products  25 us (3%)
  local copies, waits for them, and re-layouts  22.6 us (2%)
  between operations  17.5 us (2%)
  starting transfers between devices  13.3 us (1%)
    all_gather x1, waiting for transfers between devices, local(): lax.all_gather(reference_hidden, DP_VOCAB, axis=0, tiled=True)  675 us
    all_gather x5, blocking collectives, all_in_one(): both, at, found = (lax.all_gather(jnp.concatenate(lines), axis), 0, {})  103 us
    all_gather x1, waiting for transfers between devices, local(): segment = lax.all_gather(logit_grad, DP, axis=0, tiled=True)  50.3 us
    all_to_all x1, waiting for transfers between devices, sum_at_owner(): tiles = lax.all_to_all(in_blocks(value, dim, peers), axis, 0, 0, tiled=True)  44.1 us
    all_to_all x1, blocking collectives, local(): lax.all_to_all(policy_hidden, DP, split_axis=1, concat_axis=0, tiled=True)  30.3 us
  transfers between devices with their start and end apart: 4, of which 3 were waited for; matrix products, arithmetic and copies ran while one was open for 4% of the time, Pallas kernels for 0%

commit v1 on v0

--- a/solution.py
+++ b/solution.py
@@ -142,7 +142,9 @@
     logit_grad = (
         token_scale[None, :] * (onehot - jnp.exp(policy_logits - policy_total[None, :]))
     ).astype(jnp.bfloat16)
-    segment = lax.all_gather(logit_grad, DP, axis=0, tiled=True)
+    segment = jnp.concatenate(
+        lax.all_to_all(jnp.stack([logit_grad] * lax.axis_size(DP)), DP, 0, 0), axis=0
+    )
     weight_block = policy_weight
     column_grad = lax.dot_general(
         columns, segment, (((0,), (1,)), ((), ())), preferred_element_type=jnp.float32

time: 991 us -> 1050 us (1.060)
  blocking collectives: 134 us -> 230 us
  waiting for transfers between devices: 771 us -> 718 us
  local copies, waits for them, and re-layouts: 22.6 us -> 37.1 us
    all_to_all x0 -> x1, blocking collectives: none -> 96.7 us  [local(): lax.all_to_all(jnp.stack([logit_grad] * lax.axis_size(DP)), DP, 0, 0)]
    all_gather x1 -> x0, waiting for transfers between devices: 50.3 us -> none  [local(): segment = lax.all_gather(logit_grad, DP, axis=0, tiled=True)]
  transfers between devices with their start and end apart: 4 -> 3, of which waited for: 3 -> 2; matrix products, arithmetic and copies ran while one was open for 4% -> 4% of each run, Pallas kernels for 0% -> 0%
where the time goes in v1:
time: 1050 us
  waiting for transfers between devices  718 us (68%)
  blocking collectives  230 us (22%)
  local copies, waits for them, and re-layouts  37.1 us (4%)
  matrix products  25 us (2%)
  between operations  17.5 us (2%)
    all_gather x1, waiting for transfers between devices, local(): lax.all_gather(reference_hidden, DP_VOCAB, axis=0, tiled=True)  675 us
    all_gather x5, blocking collectives, all_in_one(): both, at, found = (lax.all_gather(jnp.concatenate(lines), axis), 0, {})  103 us
    all_to_all x1, blocking collectives, local(): lax.all_to_all(jnp.stack([logit_grad] * lax.axis_size(DP)), DP, 0, 0)  96.7 us
    all_to_all x1, waiting for transfers between devices, sum_at_owner(): tiles = lax.all_to_all(in_blocks(value, dim, peers), axis, 0, 0, tiled=True)  41.5 us
    all_to_all x1, blocking collectives, local(): lax.all_to_all(policy_hidden, DP, split_axis=1, concat_axis=0, tiled=True)  30.3 us
  transfers between devices with their start and end apart: 3, of which 2 were waited for; matrix products, arithmetic and copies ran while one was open for 4% of the time, Pallas kernels for 0%

profile of v1, /device:TPU:38, one launch (start us, length us, event | category | flops | bytes accessed | tf_op | source)
XLA Modules:
  0.0 1045.2 jit_solution(8980811187186283858)
XLA Ops:
  8.1 0.7 all-gather.13.cloned.1.call-update
  8.7 0.0 reduce-scatter.2.cloned.1.call-start
  8.8 2.3 copy.28
  11.1 30.3 %all_to_all.29 = bf16[128,8,512]{0,2,1:T(8,128)(2,1)S(1)} all-to-all(bf16[128,8,512]{0,2,1:T(8,128)(2,1)} %bitcast.461), channel_id=1, replica_groups=mesh['dp_0'=4,'dp_1'=2,'vocab_0'=2,'vocab_1'=4,'vocab_2'=4] {'dp_0','dp_1'}, dimensions={1} | all-to-all | bytes 2097152 | tf_op jit(solution)/shard_map/all_to_all | solution.py:102
  41.3 1.3 copy.29
  42.6 6.9 fusion.96
  49.5 0.6 copy-done.5
  50.2 0.1 slice.613
  50.3 0.1 slice.516
  50.4 675.5 %all-gather.13.cloned.1.call-done = bf16[256,4,4096]{2,1,0:T(4,128)(2,1)} async-done(((bf16[1,4,4096]{2,1,0:T(4,128)(2,1)}), bf16[256,4,4096]{2,1,0:T(4,128)(2,1)}) %all-gather.13.cloned.1.call-update) | async-done | bytes 8388624 | tf_op jit(solution)/shard_map/all_gather | solution.py:104
  725.9 12.5 %reshape.1604 = bf16[1024,4096]{1,0:T(8,128)(2,1)} reshape(bf16[256,4,4096]{2,1,0:T(4,128)(2,1)} %all-gather.13.cloned.1.call-done) | data formatting | bytes 16777216
  738.4 6.4 fusion.95
  744.8 0.3 select_reduce_fusion
  745.1 1.4 reduce_max.18
  746.5 1.5 select_reduce_fusion.1
  748.0 0.1 concatenate.15
  748.1 59.3 %all-gather.6 = f32[4,6,1024]{2,1,0:T(8,128)S(1)} all-gather(f32[1,6,1024]{2,1,0:T(8,128)S(1)} %bitcast.464), channel_id=2, replica_groups=mesh['dp_0'=4,'dp_1'=2,'vocab_0'=2,'vocab_1'=4,'vocab_2'=4] {'dp_0'}, dimensions={0}, use_global_device_ids=true | all-gather | bytes 122880 | tf_op jit(solution)/shard_map/all_gather | solution.py:23
  807.4 0.1 fusion.41
  807.5 0.1 concatenate.16
  807.6 1.9 all-gather.7
  809.5 0.1 concatenate.17
  809.5 8.5 all-gather.8
  818.1 0.1 concatenate.18
  818.1 21.7 %all-gather.9 = f32[4,6,1024]{2,1,0:T(8,128)S(1)} all-gather(f32[1,6,1024]{2,1,0:T(8,128)S(1)} %bitcast.467), channel_id=5, replica_groups=mesh['dp_0'=4,'dp_1'=2,'vocab_0'=2,'vocab_1'=4,'vocab_2'=4] {'vocab_1'}, dimensions={0}, use_global_device_ids=true | all-gather | bytes 122880 | tf_op jit(solution)/shard_map/all_gather | solution.py:23
  839.9 0.1 fusion.5
  840.0 0.1 concatenate.19
  840.0 12.1 %all-gather.10 = f32[4,6,1024]{2,1,0:T(8,128)S(1)} all-gather(f32[1,6,1024]{2,1,0:T(8,128)S(1)} %bitcast.468), channel_id=6, replica_groups=mesh['dp_0'=4,'dp_1'=2,'vocab_0'=2,'vocab_1'=4,'vocab_2'=4] {'vocab_2'}, dimensions={0}, use_global_device_ids=true | all-gather | bytes 122880 | tf_op jit(solution)/shard_map/all_gather | solution.py:23
  852.1 0.1 fusion.94
  852.2 0.1 reshape.1577
  852.3 0.1 reduce_sum.76
  852.4 0.7 gather_fusion.1
  853.1 0.7 gather_fusion
  853.8 0.6 fusion.85
  854.4 0.1 subtract_reduce_fusion
  854.5 0.1 broadcast_in_dim.51
  854.6 0.1 reshape.1578
  854.6 1.1 multiply_convert_fusion
  855.7 1.2 copy.30
  857.0 0.3 stack.2
  857.2 96.7 %all_to_all.30 = bf16[8,256,1024]{1,2,0:T(8,128)(2,1)} all-to-all(bf16[8,256,1024]{1,2,0:T(8,128)(2,1)S(1)} %stack.2), channel_id=1, replica_groups=mesh['dp_0'=4,'dp_1'=2,'vocab_0'=2,'vocab_1'=4,'vocab_2'=4] {'dp_0','dp_1'}, dimensions={0} | all-to-all | bytes 8388608 | tf_op jit(solution)/shard_map/all_to_all | solution.py:146
  954.0 6.4 copy.31
  960.4 6.5 copy.32
  966.9 5.9 fusion.1
  972.9 9.4 all-to-all-start.2
  982.9 5.9 fusion
  988.8 3.9 copy.33
  992.7 41.5 %all-to-all-done.2 = f32[32,32,512]{2,1,0:T(8,128)} async-done(((f32[32,32,512]{2,1,0:T(8,128)}), f32[32,32,512]{2,1,0:T(8,128)}, u32[]{:S(2)}, u32[]{:S(2)}) %all-to-all-start.2) | async-done | bytes 2097184 | tf_op jit(solution)/shard_map/all_to_all | solution.py:49
  1034.2 2.4 reduce_sum.78
  (28 shorter events, 0.4 us)
Async XLA Ops:
  8.0 34.6 %copy-start = (bf16[512,2048]{1,0:T(8,128)(2,1)S(1)}, bf16[512,2048]{1,0:T(8,128)(2,1)}, u32[]{:S(2)}) copy-start(bf16[512,2048]{1,0:T(8,128)(2,1)} %param.8) | copy-start | bytes 6291460
  8.0 717.9 %all-gather.13.cloned.1.call-start = ((), (), s32[]{:S(2)}) async-start(), calls=%async_computation.5 | async-start | bytes 8421376 | tf_op jit(solution)/shard_map/all_gather | solution.py:104
  8.7 736.4 %reduce-scatter.2.cloned.1.call-start = ((), (), s32[]{:S(2)}) async-start(), calls=%async_computation.4 | async-start | bytes 9437184 | tf_op jit(solution)/shard_map/reduce_scatter | solution.py:113
  49.5 0.7 copy-start.5
  49.5 0.9 copy-start.4
  744.8 107.4 %copy-start.3 = (s32[1024]{0:T(1024)S(1)}, s32[1024]{0:T(1024)}, u32[]{:S(2)}) copy-start(s32[1024]{0:T(1024)} %param.12) | copy-start | bytes 12292
  745.1 109.5 %copy-start.1 = (f32[256,1024]{1,0:T(8,128)S(1)}, f32[256,1024]{1,0:T(8,128)}, u32[]{:S(2)}) copy-start(f32[256,1024]{1,0:T(8,128)} %reduce-scatter.2.cloned.1.call-done) | copy-start | bytes 3145732
  972.9 10.0 copy-start.2
  972.9 61.4 %all-to-all-start.2 = ((f32[32,32,512]{2,1,0:T(8,128)}), f32[32,32,512]{2,1,0:T(8,128)}, u32[]{:S(2)}, u32[]{:S(2)}) async-start(f32[32,32,512]{2,1,0:T(8,128)} %fusion.1), calls=%async_computation.3 | async-start | bytes 4194304 | tf_op jit(solution)/shard_map/all_to_all | solution.py:49
Sparse Core Ops, SparseCore 0:
  10.7 715.1 all-gather.12
Sparse Core Ops, SparseCore 1:
  49.6 93.9 reduce-scatter.1
